TPU v7x, 32 devices: a whole 2x2x4 slice. The times are simulated.
32 devices in a mesh: face: 2 (over y), fy: 4 (over x, core), fx: 4 (over z).
Axes of the slice: x: 2, y: 2, z: 4, core: 2. Of those that a mesh axis runs over, the one named last changes fastest.
Arguments:
- state: float32 [6, 32, 32, 192], P('face', 'fy', 'fx'), may hold values from -6 to 6
- jacobian: float32 [6, 32, 32], P('face', 'fy', 'fx'), may hold values from 0.5 to 2
- metric_diag: float32 [2, 6, 32, 32], P(None, 'face', 'fy', 'fx'), may hold values from 0.6 to 1.4
- metric_cross: float32 [6, 32, 32], P('face', 'fy', 'fx'), may hold values from -0.3 to 0.3
- coriolis: float32 [6, 32, 32], P('face', 'fy', 'fx'), may hold values from -2 to 2
- nbr_face: int32 [6, 4], replicated, may hold values from 0 to 5, as said below
- nbr_edge: int32 [6, 4], replicated, may hold values from 0 to 3, as said below
Outputs:
- updated: float32 [6, 32, 32, 192], P('face', 'fy', 'fx')
Inputs may be any that keep to these rules, and one draw needn't show every extreme that they name: Edge e of a face is 0 south (row 0), 1 east (last column), 2 north (last row), 3 west (column 0). Edge e of face f is glued to edge nbr_edge[f, e] of face nbr_face[f, e], and that edge back to it; the 6 faces are glued as the surface of a cube, three faces at each corner, the two glued edges running in opposite senses when both are read counterclockwise. `nbr_edge`: see nbr_face.
All inputs are finite; a program needn't handle non-finite values.
Results may differ from a plain program's by a relative error of at most 0.0001.
Values sent between devices are 32-bit elements; how exact they have to be, the bound alone decides.
A program may use at most 64 MiB of HBM per device.

v0:
```python
import jax
import jax.numpy as jnp
import numpy as np
from jax import lax
from jax.sharding import PartitionSpec as P

time_step = 0.05
hyper_coeff = 0.0005


def padded(cells, sides, width):
    for axis, dim in sides:
        count = lax.axis_size(axis)
        ends = count - 1
        head = lax.slice_in_dim(cells, 0, width, axis=dim)
        tail = lax.slice_in_dim(cells, cells.shape[dim] - width, cells.shape[dim], axis=dim)
        cells = jnp.concatenate(
            [
                lax.ppermute(tail, axis, [(i, (i + 1) % count) for i in range(ends)]),
                cells,
                lax.ppermute(head, axis, [((i + 1) % count, i) for i in range(ends)]),
            ],
            axis=dim,
        )
    return cells


def deriv_table():
    gll_nodes = np.array([-1.0, -1.0 / np.sqrt(5.0), 1.0 / np.sqrt(5.0), 1.0])
    bary_weights = np.ones(4)
    for j in range(4):
        for m in range(4):
            if m != j:
                bary_weights[j] = bary_weights[j] / (gll_nodes[j] - gll_nodes[m])
    matrix = np.zeros((4, 4))
    for i in range(4):
        for j in range(4):
            if i != j:
                matrix[i, j] = bary_weights[j] / bary_weights[i] / (gll_nodes[i] - gll_nodes[j])
        matrix[i, i] = -np.sum(matrix[i])
    return matrix


def along_x(values):
    face_count, row_count, col_count, chan_count = values.shape
    blocks = values.reshape(face_count, row_count, col_count // 4, 4, chan_count)
    result = jnp.einsum(
        "jk,abekc->abejc",
        jnp.asarray(deriv_table(), jnp.float32),
        blocks,
        precision=lax.Precision.HIGHEST,
    )
    return result.reshape(values.shape)


def along_y(values):
    face_count, row_count, col_count, chan_count = values.shape
    blocks = values.reshape(face_count, row_count // 4, 4, col_count, chan_count)
    result = jnp.einsum(
        "ik,aekxc->aeixc",
        jnp.asarray(deriv_table(), jnp.float32),
        blocks,
        precision=lax.Precision.HIGHEST,
    )
    return result.reshape(values.shape)


def mass_of(jacobian):
    weights = jnp.asarray([1.0 / 6.0, 5.0 / 6.0, 5.0 / 6.0, 1.0 / 6.0], jnp.float32)
    row_weight = jnp.tile(weights, jacobian.shape[1] // 4)
    col_weight = jnp.tile(weights, jacobian.shape[2] // 4)
    return jacobian * row_weight[None, :, None] * col_weight[None, None, :]


def tendency(state, geometry, planet):
    volume, metric_xx, metric_yy, metric_xy = geometry
    levels = state.shape[-1] // 3
    wind_u = state[..., :levels]
    wind_v = state[..., levels : 2 * levels]
    temper = state[..., 2 * levels :]
    contra_u = metric_xx * wind_u + metric_xy * wind_v
    contra_v = metric_xy * wind_u + metric_yy * wind_v
    energy = 0.5 * (wind_u * contra_u + wind_v * contra_v) + temper
    xderivs = along_x(jnp.concatenate([wind_v, temper, energy], -1))
    yderivs = along_y(jnp.concatenate([wind_u, temper, energy], -1))
    absolute = (xderivs[..., :levels] - yderivs[..., :levels]) / volume + planet
    tend_u = absolute * volume * contra_v - xderivs[..., 2 * levels :]
    tend_v = -absolute * volume * contra_u - yderivs[..., 2 * levels :]
    tend_t = -(
        contra_u * xderivs[..., levels : 2 * levels] + contra_v * yderivs[..., levels : 2 * levels]
    )
    return state + time_step * jnp.concatenate([tend_u, tend_v, tend_t], -1)


def laplace(values, geometry):
    volume, metric_xx, metric_yy, metric_xy = geometry
    grad_x = along_x(values)
    grad_y = along_y(values)
    flux_x = volume * (metric_xx * grad_x + metric_xy * grad_y)
    flux_y = volume * (metric_xy * grad_x + metric_yy * grad_y)
    return (along_x(flux_x) + along_y(flux_y)) / volume


def combine(values, axis):
    length = values.shape[axis] - 2
    positions = jnp.arange(length)
    leading = (positions % 4 == 0).astype(jnp.float32)
    trailing = (positions % 4 == 3).astype(jnp.float32)
    broad_shape = [1, 1, 1, 1]
    broad_shape[axis] = length
    leading = leading.reshape(broad_shape)
    trailing = trailing.reshape(broad_shape)
    middle = lax.slice_in_dim(values, 1, length + 1, axis=axis)
    previous = lax.slice_in_dim(values, 0, length, axis=axis)
    following = lax.slice_in_dim(values, 2, length + 2, axis=axis)
    return middle + leading * previous + trailing * following


def rotate(segment, quarter, levels):
    cosine = ((quarter == 0).astype(jnp.float32) - (quarter == 2).astype(jnp.float32))[..., None]
    sine_part = ((quarter == 1).astype(jnp.float32) - (quarter == 3).astype(jnp.float32))[..., None]
    wind_u = segment[..., :levels]
    wind_v = segment[..., levels : 2 * levels]
    return jnp.concatenate(
        [
            cosine * wind_u - sine_part * wind_v,
            sine_part * wind_u + cosine * wind_v,
            segment[..., 2 * levels :],
        ],
        -1,
    )


def in_face(values):
    across = combine(padded(values, (("fx", 2),), 1), 2)
    return combine(padded(across, (("fy", 1),), 1), 1)


def place_pieces(
    got_flat,
    got_tall,
    vector,
    nbr_edge,
    flat_edge,
    tall_edge,
    on_south,
    on_west,
    flat_start,
    tall_start,
    face_local,
    side_nodes,
    chan_count,
    levels,
):
    edge_ids = jnp.arange(4, dtype=jnp.int32)
    flat_target = nbr_edge[:, flat_edge]
    tall_target = nbr_edge[:, tall_edge]
    if vector:
        got_flat = rotate(got_flat, ((flat_target - flat_edge + 2) % 4)[None, :, None], levels)
        got_tall = rotate(got_tall, ((tall_target - tall_edge + 2) % 4)[None, :, None], levels)
    got_flat = jnp.where(on_south, got_flat[:, :, ::-1], got_flat)
    got_tall = jnp.where(on_west, got_tall, got_tall[:, :, ::-1])
    flat_pick = (flat_target[:, None] == edge_ids[None, :]).astype(jnp.float32)
    tall_pick = (tall_target[:, None] == edge_ids[None, :]).astype(jnp.float32)
    flat_rims = jnp.einsum("se,gsjc->gejc", flat_pick, got_flat, precision=lax.Precision.HIGHEST)
    tall_rims = jnp.einsum("se,gsjc->gejc", tall_pick, got_tall, precision=lax.Precision.HIGHEST)
    empty_rims = jnp.zeros((face_local, 4, side_nodes, chan_count), jnp.float32)
    rim_strips = lax.dynamic_update_slice(empty_rims, flat_rims, (0, 0, flat_start, 0))
    return rim_strips + lax.dynamic_update_slice(empty_rims, tall_rims, (0, 0, tall_start, 0))


def outgoing(
    summed, nbr_face, face_ids, flat_edge, tall_edge, on_south, on_west, flat_live, tall_live
):
    row_count = summed.shape[1]
    col_count = summed.shape[2]
    all_faces = jnp.arange(nbr_face.shape[0], dtype=jnp.int32)
    flat_piece = jnp.where(on_south, summed[:, 0], summed[:, row_count - 1])
    tall_piece = jnp.where(on_west, summed[:, :, 0], summed[:, :, col_count - 1])
    flat_dest = nbr_face[face_ids, flat_edge]
    tall_dest = nbr_face[face_ids, tall_edge]
    flat_send = ((all_faces[:, None] == flat_dest[None, :]) & flat_live).astype(jnp.float32)
    tall_send = ((all_faces[:, None] == tall_dest[None, :]) & tall_live).astype(jnp.float32)
    return (
        flat_send[:, :, None, None] * flat_piece[None],
        tall_send[:, :, None, None] * tall_piece[None],
    )


def assemble(values, vector, nbr_face, nbr_edge):
    summed = in_face(values)
    face_local, row_count, col_count, chan_count = summed.shape
    levels = chan_count // 3
    row_index = lax.axis_index("fy")
    col_index = lax.axis_index("fx")
    side_nodes = row_count * lax.axis_size("fy")
    face_ids = lax.axis_index("face") * face_local + jnp.arange(face_local, dtype=jnp.int32)
    on_south = row_index == 0
    on_north = row_index == lax.axis_size("fy") - 1
    on_west = col_index == 0
    on_east = col_index == lax.axis_size("fx") - 1
    flat_live = on_south | on_north
    tall_live = on_west | on_east
    flat_edge = jnp.where(on_south, 0, 2).astype(jnp.int32)
    tall_edge = jnp.where(on_west, 3, 1).astype(jnp.int32)
    flat_start = jnp.where(
        on_south, side_nodes - (col_index + 1) * col_count, col_index * col_count
    )
    tall_start = jnp.where(on_west, row_index * row_count, side_nodes - (row_index + 1) * row_count)
    send_flat, send_tall = outgoing(
        summed, nbr_face, face_ids, flat_edge, tall_edge, on_south, on_west, flat_live, tall_live
    )
    got_flat, got_tall = (
        lax.all_to_all(send_flat, "face", split_axis=0, concat_axis=1, tiled=True),
        lax.all_to_all(send_tall, "face", split_axis=0, concat_axis=1, tiled=True),
    )
    rim_strips = place_pieces(
        got_flat,
        got_tall,
        vector,
        nbr_edge,
        flat_edge,
        tall_edge,
        on_south,
        on_west,
        flat_start,
        tall_start,
        face_local,
        side_nodes,
        chan_count,
        levels,
    )
    flat_lines = jnp.stack([rim_strips[:, 0], rim_strips[:, 2, ::-1]], axis=1)
    flat_lines = flat_lines.reshape(face_local, 2, lax.axis_size("fx"), col_count, chan_count)
    tall_lines = jnp.stack([rim_strips[:, 1], rim_strips[:, 3, ::-1]], axis=1)
    tall_lines = tall_lines.reshape(face_local, 2, lax.axis_size("fy"), row_count, chan_count)
    flat_whole = lax.psum(flat_lines, "fy")
    tall_whole = lax.psum(tall_lines, "fx")
    flat_block = lax.psum_scatter(flat_whole, "fx", scatter_dimension=2, tiled=True)
    tall_block = lax.psum_scatter(tall_whole, "fy", scatter_dimension=2, tiled=True)
    flat_add = jnp.where(on_south, flat_block[:, 0, 0], flat_block[:, 1, 0])
    tall_add = jnp.where(on_west, tall_block[:, 1, 0], tall_block[:, 0, 0])
    result = summed.at[:, 0].add(jnp.where(on_south, flat_add, 0.0))
    result = result.at[:, row_count - 1].add(jnp.where(on_north, flat_add, 0.0))
    result = result.at[:, :, 0].add(jnp.where(on_west, tall_add, 0.0))
    result = result.at[:, :, col_count - 1].add(jnp.where(on_east, tall_add, 0.0))
    return result


def per_device(state, jacobian, metric_diag, metric_cross, coriolis, nbr_face, nbr_edge):
    node_mass = mass_of(jacobian)[..., None]
    total_mass = assemble(node_mass, False, nbr_face, nbr_edge)
    geometry = (
        jacobian[..., None],
        metric_diag[0][..., None],
        metric_diag[1][..., None],
        metric_cross[..., None],
    )
    raw = tendency(state, geometry, coriolis[..., None])
    sectioned = assemble(node_mass * raw, True, nbr_face, nbr_edge) / total_mass
    first_lap = (
        assemble(node_mass * laplace(sectioned, geometry), True, nbr_face, nbr_edge) / total_mass
    )
    second_lap = (
        assemble(node_mass * laplace(first_lap, geometry), True, nbr_face, nbr_edge) / total_mass
    )
    return sectioned - hyper_coeff * second_lap


def solution(mesh):
    return jax.shard_map(
        per_device,
        mesh=mesh,
        in_specs=(
            P("face", "fy", "fx", None),
            P("face", "fy", "fx"),
            P(None, "face", "fy", "fx"),
            P("face", "fy", "fx"),
            P("face", "fy", "fx"),
            P(),
            P(),
        ),
        out_specs=P("face", "fy", "fx", None),
        check_vma=False,
    )
```

profile of v0, /device:TPU:0, one launch (start us, length us, event | category | flops | bytes accessed | tf_op | source)
XLA Modules:
  0.0 370.9 jit_solution(3466996314126042414)
XLA Ops:
  7.4 0.8 fusion.161
  8.1 1.0 slice.770
  13.0 1.3 collective-permute-start.1
  14.4 5.6 %collective-permute-start = (f32[3,8,1,192]{3,2,0,1:T(1,128)S(1)}, f32[3,8,1,192]{3,2,0,1:T(1,128)S(1)}, u32[]{:S(2)}, u32[]{:S(2)}) collective-permute-start(f32[3,8,1,192]{3,2,0,1:T(1,128)S(1)} %slice.902), channel_id=1, source_target_pairs={{0,1},{1,2},{2,3},{4,5},{5,6},{6,7},{8,9},{9,10},{10,11},{12,13},{... | collective-permute-start | bytes 55304 | tf_op jit(solution)/shard_map/ppermute | solution.py:19
  20.1 1.3 collective-permute-start.5
  21.4 4.5 %collective-permute-start.4 = (f32[3,8,1,1]{2,1,0,3:T(8,128)S(1)}, f32[3,8,1,1]{2,1,0,3:T(8,128)S(1)}, u32[]{:S(2)}, u32[]{:S(2)}) collective-permute-start(f32[3,8,1,1]{2,1,0,3:T(8,128)S(1)} %get-tuple-element.262), channel_id=1, source_target_pairs={{0,1},{1,2},{2,3},{4,5},{5,6},{6,7},{8,9},{9,10},{10,11},{12,13},{... | collective-permute-start | bytes 296 | tf_op jit(solution)/shard_map/ppermute | solution.py:19
  31.1 1.3 collective-permute-start.7
  32.4 3.0 collective-permute-start.6
  35.5 0.8 collective-permute-done.6
  37.2 3.2 all-to-all-start.2
  41.1 3.1 all-to-all-done.2
  44.3 3.2 all-to-all-start.3
  47.6 3.7 all-to-all-done.3
  52.8 1.3 collective-permute-start.3
  54.1 3.0 collective-permute-start.2
  57.2 13.3 %all-reduce.4 = f32[3,2,4,8,1]{3,1,4,0,2:T(2,128)S(1)} all-reduce(f32[3,2,4,8,1]{3,1,4,0,2:T(2,128)S(1)} %copy.284), channel_id=5, replica_groups=mesh['face'=2,'fy'=4,'fx'=4] {'fy'}, use_global_device_ids=true, to_apply=%region_7.8.clone | all-reduce | flops 192 | bytes 1536
  70.7 0.7 broadcast_multiply_fusion.5
  71.4 3.4 all-to-all-start
  74.9 0.8 broadcast_multiply_fusion.4
  75.7 3.7 %all-to-all-done = f32[6,3,8,192]{3,2,1,0:T(8,128)S(1)} async-done(((f32[6,3,8,192]{3,2,1,0:T(8,128)}), f32[6,3,8,192]{3,2,1,0:T(8,128)S(1)}, u32[]{:S(2)}, u32[]{:S(2)}) %all-to-all-start) | async-done | bytes 110624 | tf_op jit(solution)/shard_map/all_to_all | solution.py:214
  79.4 3.4 all-to-all-start.1
  83.3 4.1 %all-to-all-done.1 = f32[6,3,8,192]{3,2,1,0:T(8,128)S(1)} async-done(((f32[6,3,8,192]{3,2,1,0:T(8,128)}), f32[6,3,8,192]{3,2,1,0:T(8,128)S(1)}, u32[]{:S(2)}, u32[]{:S(2)}) %all-to-all-start.1) | async-done | bytes 110624 | tf_op jit(solution)/shard_map/all_to_all | solution.py:215
  88.9 0.7 copy.270
  91.5 33.0 %all-reduce.13.cloned.1.call-done = f32[3,2,4,8,192]{4,3,0,2,1:T(8,128)} async-done(((f32[3,2,4,8,192]{4,3,0,2,1:T(8,128)}), f32[3,2,4,8,192]{4,3,0,2,1:T(8,128)}) %all-reduce.13.cloned.1.call-update) | async-done | bytes 147472
  124.5 1.4 constant_dynamic-slice_fusion.6
  125.9 0.8 copy.277
  126.8 18.5 %all-reduce.7 = (f32[3,2,1,8,192]{4,1,3,2,0:T(2,128)S(1)}, f32[3,2,4,8,1]{3,1,4,0,2:T(2,128)S(1)}, f32[3,2,1,8,1]{3,1,4,0,2:T(2,128)S(1)}) all-reduce(f32[3,2,1,8,192]{4,1,3,2,0:T(2,128)S(1)} %copy.277, f32[3,2,4,8,1]{3,1,4,0,2:T(2,128)S(1)} %copy.281, ...), channel_id=1, replica_groups=mesh['face'=2,'fy'=4,'fx'=4] {'fx'}, use_global_device_ids=true, to_apply=%region_2.3 | all-reduce | flops 9456 | bytes 75648 | tf_op jit(solution)/shard_map/psum | solution.py:238
  145.9 10.7 %all-reduce.8 = (f32[3,2,1,8,192]{4,3,0,2,1:T(8,128)S(1)}, f32[3,2,1,8,1]{3,1,4,0,2:T(2,128)S(1)}) all-reduce(f32[3,2,1,8,192]{4,3,0,2,1:T(8,128)S(1)} %constant_dynamic-slice_fusion.6, f32[3,2,1,8,1]{3,1,4,0,2:T(2,128)S(1)} %constant_dynamic-slice_fusion.5), channel_id=1, replica_groups=mesh['face'=2,'fy'=4,'fx'=4] {'fy'}, use_global_device_ids=true, to_apply=%region_0.1 | all-reduce | flops 9264 | bytes 74112 | tf_op jit(solution)/shard_map/psum | solution.py:237
  160.6 1.3 collective-permute-start.9
  161.9 4.5 %collective-permute-start.8 = (f32[3,8,1,192]{3,2,0,1:T(1,128)S(1)}, f32[3,8,1,192]{3,2,0,1:T(1,128)S(1)}, u32[]{:S(2)}, u32[]{:S(2)}) collective-permute-start(f32[3,8,1,192]{3,2,0,1:T(1,128)S(1)} %get-tuple-element.230), channel_id=1, source_target_pairs={{0,1},{1,2},{2,3},{4,5},{5,6},{6,7},{8,9},{9,10},{10,11},{12,13},{... | collective-permute-start | bytes 55304 | tf_op jit(solution)/shard_map/ppermute | solution.py:19
  166.4 1.5 collective-permute-done.8
  168.0 1.3 collective-permute-start.11
  169.3 3.2 collective-permute-start.10
  173.4 0.7 broadcast_multiply_fusion.3
  174.1 3.4 all-to-all-start.4
  177.6 0.8 broadcast_multiply_fusion.2
  178.3 4.0 %all-to-all-done.4 = f32[6,3,8,192]{3,2,1,0:T(8,128)S(1)} async-done(((f32[6,3,8,192]{3,2,1,0:T(8,128)}), f32[6,3,8,192]{3,2,1,0:T(8,128)S(1)}, u32[]{:S(2)}, u32[]{:S(2)}) %all-to-all-start.4) | async-done | bytes 110624 | tf_op jit(solution)/shard_map/all_to_all | solution.py:214
  182.3 3.4 all-to-all-start.5
  186.2 4.3 %all-to-all-done.5 = f32[6,3,8,192]{3,2,1,0:T(8,128)S(1)} async-done(((f32[6,3,8,192]{3,2,1,0:T(8,128)}), f32[6,3,8,192]{3,2,1,0:T(8,128)S(1)}, u32[]{:S(2)}, u32[]{:S(2)}) %all-to-all-start.5) | async-done | bytes 110624 | tf_op jit(solution)/shard_map/all_to_all | solution.py:215
  192.1 0.7 copy.308
  193.8 35.0 %all-reduce.15.cloned.1.call-done = f32[3,2,4,8,192]{4,3,0,2,1:T(8,128)} async-done(((f32[3,2,4,8,192]{4,3,0,2,1:T(8,128)}), f32[3,2,4,8,192]{4,3,0,2,1:T(8,128)}) %all-reduce.15.cloned.1.call-update) | async-done | bytes 147472
  228.8 1.4 constant_dynamic-slice_fusion.3
  230.3 10.5 %psum.68 = f32[3,2,1,8,192]{4,3,0,2,1:T(8,128)S(1)} all-reduce(f32[3,2,1,8,192]{4,3,0,2,1:T(8,128)S(1)} %constant_dynamic-slice_fusion.3), channel_id=1, replica_groups=mesh['face'=2,'fy'=4,'fx'=4] {'fy'}, use_global_device_ids=true, to_apply=%region_8.9 | all-reduce | flops 9216 | bytes 73728 | tf_op jit(solution)/shard_map/psum | solution.py:237
  240.9 0.8 copy.314
  241.7 18.2 %psum.69 = f32[3,2,1,8,192]{4,1,3,2,0:T(2,128)S(1)} all-reduce(f32[3,2,1,8,192]{4,1,3,2,0:T(2,128)S(1)} %copy.314), channel_id=1, replica_groups=mesh['face'=2,'fy'=4,'fx'=4] {'fx'}, use_global_device_ids=true, to_apply=%region_10.11 | all-reduce | flops 9216 | bytes 73728 | tf_op jit(solution)/shard_map/psum | solution.py:238
  263.2 1.3 collective-permute-start.13
  264.5 4.5 %collective-permute-start.12 = (f32[3,8,1,192]{3,2,0,1:T(1,128)S(1)}, f32[3,8,1,192]{3,2,0,1:T(1,128)S(1)}, u32[]{:S(2)}, u32[]{:S(2)}) collective-permute-start(f32[3,8,1,192]{3,2,0,1:T(1,128)S(1)} %get-tuple-element.226), channel_id=1, source_target_pairs={{0,1},{1,2},{2,3},{4,5},{5,6},{6,7},{8,9},{9,10},{10,11},{12,13},{... | collective-permute-start | bytes 55304 | tf_op jit(solution)/shard_map/ppermute | solution.py:19
  269.0 1.5 collective-permute-done.12
  270.6 1.3 collective-permute-start.15
  271.9 3.0 collective-permute-start.14
  275.0 0.8 collective-permute-done.14
  276.0 0.7 broadcast_multiply_fusion.1
  276.7 3.4 all-to-all-start.6
  280.2 0.8 broadcast_multiply_fusion
  280.9 4.0 %all-to-all-done.6 = f32[6,3,8,192]{3,2,1,0:T(8,128)S(1)} async-done(((f32[6,3,8,192]{3,2,1,0:T(8,128)}), f32[6,3,8,192]{3,2,1,0:T(8,128)S(1)}, u32[]{:S(2)}, u32[]{:S(2)}) %all-to-all-start.6) | async-done | bytes 110624 | tf_op jit(solution)/shard_map/all_to_all | solution.py:214
  284.9 3.4 all-to-all-start.7
  288.9 4.2 %all-to-all-done.7 = f32[6,3,8,192]{3,2,1,0:T(8,128)S(1)} async-done(((f32[6,3,8,192]{3,2,1,0:T(8,128)}), f32[6,3,8,192]{3,2,1,0:T(8,128)S(1)}, u32[]{:S(2)}, u32[]{:S(2)}) %all-to-all-start.7) | async-done | bytes 110624 | tf_op jit(solution)/shard_map/all_to_all | solution.py:215
  294.7 0.7 copy.326
  296.4 34.9 %all-reduce.17.cloned.1.call-done = f32[3,2,4,8,192]{4,3,0,2,1:T(8,128)} async-done(((f32[3,2,4,8,192]{4,3,0,2,1:T(8,128)}), f32[3,2,4,8,192]{4,3,0,2,1:T(8,128)}) %all-reduce.17.cloned.1.call-update) | async-done | bytes 147472
  331.3 1.4 constant_dynamic-slice_fusion.2
  332.8 10.5 %psum.70 = f32[3,2,1,8,192]{4,3,0,2,1:T(8,128)S(1)} all-reduce(f32[3,2,1,8,192]{4,3,0,2,1:T(8,128)S(1)} %constant_dynamic-slice_fusion.2), channel_id=1, replica_groups=mesh['face'=2,'fy'=4,'fx'=4] {'fy'}, use_global_device_ids=true, to_apply=%region_12.13 | all-reduce | flops 9216 | bytes 73728 | tf_op jit(solution)/shard_map/psum | solution.py:237
  343.4 0.8 copy.330
  344.2 18.2 %psum.71 = f32[3,2,1,8,192]{4,1,3,2,0:T(2,128)S(1)} all-reduce(f32[3,2,1,8,192]{4,1,3,2,0:T(2,128)S(1)} %copy.330), channel_id=1, replica_groups=mesh['face'=2,'fy'=4,'fx'=4] {'fx'}, use_global_device_ids=true, to_apply=%region_14.15 | all-reduce | flops 9216 | bytes 73728 | tf_op jit(solution)/shard_map/psum | solution.py:238
  362.8 0.8 multiply_subtract_fusion
  (252 shorter events, 31.3 us)
Async XLA Ops:
  7.4 19.6 %copy-start = (s32[6,4]{0,1:T(4,128)S(1)}, s32[6,4]{0,1:T(4,128)}, u32[]{:S(2)}) copy-start(s32[6,4]{0,1:T(4,128)} %param.55) | copy-start | bytes 292
  7.4 1.8 copy-start.1
  8.1 1.0 copy-start.3
  9.5 0.7 copy-start.4
  11.2 0.7 copy-start.9
  11.2 0.7 copy-start.2
  12.0 0.7 copy-start.5
  13.0 39.6 %collective-permute-start.1 = (f32[3,8,1,192]{3,2,1,0:T(1,128)S(1)}, f32[3,8,1,192]{3,2,1,0:T(1,128)S(1)}, u32[]{:S(2)}, u32[]{:S(2)}) collective-permute-start(f32[3,8,1,192]{3,2,1,0:T(1,128)S(1)} %slice.903), channel_id=1, source_target_pairs={{1,0},{2,1},{3,2},{5,4},{6,5},{7,6},{9,8},{10,9},{11,10},{13,12},{... | collective-permute-start | bytes 55304 | tf_op jit(solution)/shard_map/ppermute | solution.py:21
  14.4 38.2 %collective-permute-start = (f32[3,8,1,192]{3,2,0,1:T(1,128)S(1)}, f32[3,8,1,192]{3,2,0,1:T(1,128)S(1)}, u32[]{:S(2)}, u32[]{:S(2)}) collective-permute-start(f32[3,8,1,192]{3,2,0,1:T(1,128)S(1)} %slice.902), channel_id=1, source_target_pairs={{0,1},{1,2},{2,3},{4,5},{5,6},{6,7},{8,9},{9,10},{10,11},{12,13},{... | collective-permute-start | bytes 55304 | tf_op jit(solution)/shard_map/ppermute | solution.py:19
  20.1 10.9 %collective-permute-start.5 = (f32[3,8,1,1]{2,1,0,3:T(8,128)S(1)}, f32[3,8,1,1]{2,1,0,3:T(8,128)S(1)}, u32[]{:S(2)}, u32[]{:S(2)}) collective-permute-start(f32[3,8,1,1]{2,1,0,3:T(8,128)S(1)} %get-tuple-element.263), channel_id=1, source_target_pairs={{1,0},{2,1},{3,2},{5,4},{6,5},{7,6},{9,8},{10,9},{11,10},{13,12},{... | collective-permute-start | bytes 296 | tf_op jit(solution)/shard_map/ppermute | solution.py:21
  21.4 9.6 %collective-permute-start.4 = (f32[3,8,1,1]{2,1,0,3:T(8,128)S(1)}, f32[3,8,1,1]{2,1,0,3:T(8,128)S(1)}, u32[]{:S(2)}, u32[]{:S(2)}) collective-permute-start(f32[3,8,1,1]{2,1,0,3:T(8,128)S(1)} %get-tuple-element.262), channel_id=1, source_target_pairs={{0,1},{1,2},{2,3},{4,5},{5,6},{6,7},{8,9},{9,10},{10,11},{12,13},{... | collective-permute-start | bytes 296 | tf_op jit(solution)/shard_map/ppermute | solution.py:19
  26.0 0.7 copy-start.6
  28.3 0.7 copy-start.8
  28.9 0.7 copy-start.7
  31.1 4.3 %collective-permute-start.7 = (f32[3,1,8,1]{2,1,0,3:T(1,128)S(1)}, f32[3,1,8,1]{2,1,0,3:T(1,128)S(1)}, u32[]{:S(2)}, u32[]{:S(2)}) collective-permute-start(f32[3,1,8,1]{2,1,0,3:T(1,128)S(1)} %get-tuple-element.261), channel_id=1, source_target_pairs={{4,0},{8,4},{12,8},{5,1},{9,5},{13,9},{6,2},{10,6},{14,10},{7,3},{... | collective-permute-start | bytes 296 | tf_op jit(solution)/shard_map/ppermute | solution.py:21
  32.4 3.8 %collective-permute-start.6 = (f32[3,1,8,1]{2,1,0,3:T(1,128)S(1)}, f32[3,1,8,1]{2,1,0,3:T(1,128)S(1)}, u32[]{:S(2)}, u32[]{:S(2)}) collective-permute-start(f32[3,1,8,1]{2,1,0,3:T(1,128)S(1)} %get-tuple-element.260), channel_id=1, source_target_pairs={{0,4},{4,8},{8,12},{1,5},{5,9},{9,13},{2,6},{6,10},{10,14},{3,7},{... | collective-permute-start | bytes 296 | tf_op jit(solution)/shard_map/ppermute | solution.py:19
  37.2 7.0 %all-to-all-start.2 = ((f32[6,3,8,1]{2,3,1,0:T(1,128)}), f32[6,3,8,1]{2,3,1,0:T(1,128)S(1)}, u32[]{:S(2)}, u32[]{:S(2)}) async-start(f32[6,3,8,1]{2,3,1,0:T(1,128)} %broadcast_multiply_fusion.7), calls=%async_computation.2 | async-start | bytes 18432 | tf_op jit(solution)/shard_map/all_to_all | solution.py:214
  44.3 7.0 %all-to-all-start.3 = ((f32[6,3,8,1]{2,3,1,0:T(1,128)}), f32[6,3,8,1]{2,3,1,0:T(1,128)S(1)}, u32[]{:S(2)}, u32[]{:S(2)}) async-start(f32[6,3,8,1]{2,3,1,0:T(1,128)} %broadcast_multiply_fusion.6), calls=%async_computation.3 | async-start | bytes 18432 | tf_op jit(solution)/shard_map/all_to_all | solution.py:215
  52.8 17.7 %collective-permute-start.3 = (f32[3,1,8,192]{3,2,1,0:T(8,128)S(1)}, f32[3,1,8,192]{3,2,1,0:T(8,128)S(1)}, u32[]{:S(2)}, u32[]{:S(2)}) collective-permute-start(f32[3,1,8,192]{3,2,1,0:T(8,128)S(1)} %slice.905), channel_id=1, source_target_pairs={{4,0},{8,4},{12,8},{5,1},{9,5},{13,9},{6,2},{10,6},{14,10},{7,3},{... | collective-permute-start | bytes 55304 | tf_op jit(solution)/shard_map/ppermute | solution.py:21
  54.1 16.4 %collective-permute-start.2 = (f32[3,1,8,192]{3,2,0,1:T(8,128)S(1)}, f32[3,1,8,192]{3,2,0,1:T(8,128)S(1)}, u32[]{:S(2)}, u32[]{:S(2)}) collective-permute-start(f32[3,1,8,192]{3,2,0,1:T(8,128)S(1)} %slice.904), channel_id=1, source_target_pairs={{0,4},{4,8},{8,12},{1,5},{5,9},{9,13},{2,6},{6,10},{10,14},{3,7},{... | collective-permute-start | bytes 55304 | tf_op jit(solution)/shard_map/ppermute | solution.py:19
  71.4 8.0 %all-to-all-start = ((f32[6,3,8,192]{3,2,1,0:T(8,128)}), f32[6,3,8,192]{3,2,1,0:T(8,128)S(1)}, u32[]{:S(2)}, u32[]{:S(2)}) async-start(f32[6,3,8,192]{3,2,1,0:T(8,128)} %broadcast_multiply_fusion.5), calls=%async_computation | async-start | bytes 294912 | tf_op jit(solution)/shard_map/all_to_all | solution.py:214
  79.4 8.0 %all-to-all-start.1 = ((f32[6,3,8,192]{3,2,1,0:T(8,128)}), f32[6,3,8,192]{3,2,1,0:T(8,128)S(1)}, u32[]{:S(2)}, u32[]{:S(2)}) async-start(f32[6,3,8,192]{3,2,1,0:T(8,128)} %broadcast_multiply_fusion.4), calls=%async_computation.1 | async-start | bytes 294912 | tf_op jit(solution)/shard_map/all_to_all | solution.py:215
  82.8 41.7 %all-reduce.13.cloned.1.call-start = ((), (), s32[]{:S(2)}) async-start(), calls=%async_computation.14 | async-start | bytes 393216
  89.7 36.3 %reduce-scatter.7.cloned.1.call-start = ((), (), s32[]{:S(2)}) async-start(), calls=%async_computation.11 | async-start | bytes 245760 | tf_op jit(solution)/shard_map/reduce_scatter | solution.py:240
  160.6 5.9 %collective-permute-start.9 = (f32[3,8,1,192]{3,2,0,1:T(1,128)S(1)}, f32[3,8,1,192]{3,2,0,1:T(1,128)S(1)}, u32[]{:S(2)}, u32[]{:S(2)}) collective-permute-start(f32[3,8,1,192]{3,2,0,1:T(1,128)S(1)} %get-tuple-element.231), channel_id=1, source_target_pairs={{1,0},{2,1},{3,2},{5,4},{6,5},{7,6},{9,8},{10,9},{11,10},{13,12},{... | collective-permute-start | bytes 55304 | tf_op jit(solution)/shard_map/ppermute | solution.py:21
  161.9 6.1 %collective-permute-start.8 = (f32[3,8,1,192]{3,2,0,1:T(1,128)S(1)}, f32[3,8,1,192]{3,2,0,1:T(1,128)S(1)}, u32[]{:S(2)}, u32[]{:S(2)}) collective-permute-start(f32[3,8,1,192]{3,2,0,1:T(1,128)S(1)} %get-tuple-element.230), channel_id=1, source_target_pairs={{0,1},{1,2},{2,3},{4,5},{5,6},{6,7},{8,9},{9,10},{10,11},{12,13},{... | collective-permute-start | bytes 55304 | tf_op jit(solution)/shard_map/ppermute | solution.py:19
  168.0 4.5 %collective-permute-start.11 = (f32[3,1,8,192]{3,2,0,1:T(8,128)S(1)}, f32[3,1,8,192]{3,2,0,1:T(8,128)S(1)}, u32[]{:S(2)}, u32[]{:S(2)}) collective-permute-start(f32[3,1,8,192]{3,2,0,1:T(8,128)S(1)} %get-tuple-element.229), channel_id=1, source_target_pairs={{4,0},{8,4},{12,8},{5,1},{9,5},{13,9},{6,2},{10,6},{14,10},{7,3},{... | collective-permute-start | bytes 55304 | tf_op jit(solution)/shard_map/ppermute | solution.py:21
  169.3 3.9 %collective-permute-start.10 = (f32[3,1,8,192]{3,2,0,1:T(8,128)S(1)}, f32[3,1,8,192]{3,2,0,1:T(8,128)S(1)}, u32[]{:S(2)}, u32[]{:S(2)}) collective-permute-start(f32[3,1,8,192]{3,2,0,1:T(8,128)S(1)} %get-tuple-element.228), channel_id=1, source_target_pairs={{0,4},{4,8},{8,12},{1,5},{5,9},{9,13},{2,6},{6,10},{10,14},{3,7},{... | collective-permute-start | bytes 55304 | tf_op jit(solution)/shard_map/ppermute | solution.py:19
  174.1 8.2 %all-to-all-start.4 = ((f32[6,3,8,192]{3,2,1,0:T(8,128)}), f32[6,3,8,192]{3,2,1,0:T(8,128)S(1)}, u32[]{:S(2)}, u32[]{:S(2)}) async-start(f32[6,3,8,192]{3,2,1,0:T(8,128)} %broadcast_multiply_fusion.3), calls=%async_computation.4 | async-start | bytes 294912 | tf_op jit(solution)/shard_map/all_to_all | solution.py:214
  182.3 8.2 %all-to-all-start.5 = ((f32[6,3,8,192]{3,2,1,0:T(8,128)}), f32[6,3,8,192]{3,2,1,0:T(8,128)S(1)}, u32[]{:S(2)}, u32[]{:S(2)}) async-start(f32[6,3,8,192]{3,2,1,0:T(8,128)} %broadcast_multiply_fusion.2), calls=%async_computation.5 | async-start | bytes 294912 | tf_op jit(solution)/shard_map/all_to_all | solution.py:215
  185.7 43.1 %all-reduce.15.cloned.1.call-start = ((), (), s32[]{:S(2)}) async-start(), calls=%async_computation.15 | async-start | bytes 393216
  192.8 48.1 %reduce-scatter.9.cloned.1.call-start = ((), (), s32[]{:S(2)}) async-start(), calls=%async_computation.12 | async-start | bytes 245760 | tf_op jit(solution)/shard_map/reduce_scatter | solution.py:240
  263.2 5.9 %collective-permute-start.13 = (f32[3,8,1,192]{3,2,0,1:T(1,128)S(1)}, f32[3,8,1,192]{3,2,0,1:T(1,128)S(1)}, u32[]{:S(2)}, u32[]{:S(2)}) collective-permute-start(f32[3,8,1,192]{3,2,0,1:T(1,128)S(1)} %get-tuple-element.227), channel_id=1, source_target_pairs={{1,0},{2,1},{3,2},{5,4},{6,5},{7,6},{9,8},{10,9},{11,10},{13,12},{... | collective-permute-start | bytes 55304 | tf_op jit(solution)/shard_map/ppermute | solution.py:21
  264.5 6.1 %collective-permute-start.12 = (f32[3,8,1,192]{3,2,0,1:T(1,128)S(1)}, f32[3,8,1,192]{3,2,0,1:T(1,128)S(1)}, u32[]{:S(2)}, u32[]{:S(2)}) collective-permute-start(f32[3,8,1,192]{3,2,0,1:T(1,128)S(1)} %get-tuple-element.226), channel_id=1, source_target_pairs={{0,1},{1,2},{2,3},{4,5},{5,6},{6,7},{8,9},{9,10},{10,11},{12,13},{... | collective-permute-start | bytes 55304 | tf_op jit(solution)/shard_map/ppermute | solution.py:19
  270.6 4.3 %collective-permute-start.15 = (f32[3,1,8,192]{3,2,0,1:T(8,128)S(1)}, f32[3,1,8,192]{3,2,0,1:T(8,128)S(1)}, u32[]{:S(2)}, u32[]{:S(2)}) collective-permute-start(f32[3,1,8,192]{3,2,0,1:T(8,128)S(1)} %get-tuple-element.225), channel_id=1, source_target_pairs={{4,0},{8,4},{12,8},{5,1},{9,5},{13,9},{6,2},{10,6},{14,10},{7,3},{... | collective-permute-start | bytes 55304 | tf_op jit(solution)/shard_map/ppermute | solution.py:21
  271.9 3.9 %collective-permute-start.14 = (f32[3,1,8,192]{3,2,0,1:T(8,128)S(1)}, f32[3,1,8,192]{3,2,0,1:T(8,128)S(1)}, u32[]{:S(2)}, u32[]{:S(2)}) collective-permute-start(f32[3,1,8,192]{3,2,0,1:T(8,128)S(1)} %get-tuple-element.224), channel_id=1, source_target_pairs={{0,4},{4,8},{8,12},{1,5},{5,9},{9,13},{2,6},{6,10},{10,14},{3,7},{... | collective-permute-start | bytes 55304 | tf_op jit(solution)/shard_map/ppermute | solution.py:19
  276.7 8.2 %all-to-all-start.6 = ((f32[6,3,8,192]{3,2,1,0:T(8,128)}), f32[6,3,8,192]{3,2,1,0:T(8,128)S(1)}, u32[]{:S(2)}, u32[]{:S(2)}) async-start(f32[6,3,8,192]{3,2,1,0:T(8,128)} %broadcast_multiply_fusion.1), calls=%async_computation.6 | async-start | bytes 294912 | tf_op jit(solution)/shard_map/all_to_all | solution.py:214
  284.9 8.2 %all-to-all-start.7 = ((f32[6,3,8,192]{3,2,1,0:T(8,128)}), f32[6,3,8,192]{3,2,1,0:T(8,128)S(1)}, u32[]{:S(2)}, u32[]{:S(2)}) async-start(f32[6,3,8,192]{3,2,1,0:T(8,128)} %broadcast_multiply_fusion), calls=%async_computation.7 | async-start | bytes 294912 | tf_op jit(solution)/shard_map/all_to_all | solution.py:215
  288.4 43.0 %all-reduce.17.cloned.1.call-start = ((), (), s32[]{:S(2)}) async-start(), calls=%async_computation.16 | async-start | bytes 393216
  295.4 48.0 %reduce-scatter.11.cloned.1.call-start = ((), (), s32[]{:S(2)}) async-start(), calls=%async_computation.13 | async-start | bytes 245760 | tf_op jit(solution)/shard_map/reduce_scatter | solution.py:240
Sparse Core Ops, SparseCore 0:
  89.8 34.6 all-reduce.12
  192.9 35.8 all-reduce.14
  295.5 35.7 all-reduce.16
Sparse Core Ops, SparseCore 1:
  92.6 19.4 reduce-scatter.6
  195.7 20.6 reduce-scatter.8
  298.3 20.6 reduce-scatter.10
where the time goes:
time: 373 us; the launch traced here: 371 us
  waiting for transfers between devices  139 us (37%)
  blocking collectives  99.7 us (27%)
  starting transfers between devices  69.1 us (19%)
  local copies, waits for them, and re-layouts  26.4 us (7%)
  between operations  16.4 us (4%)
  other arithmetic  12.6 us (3%)
  matrix products  7.16 us (2%)
    unnamed x9, waiting for transfers between devices  103 us
    psum x3, blocking collectives, assemble(): tall_whole = lax.psum(tall_lines, 'fx')  54.8 us
    psum x3, blocking collectives, assemble(): flat_whole = lax.psum(flat_lines, 'fy')  31.7 us
    ppermute x8, starting transfers between devices, padded(): lax.ppermute(tail, axis, [(i, (i + 1) % count) for i in range(ends)])  31.5 us
    all_to_all x4, waiting for transfers between devices, assemble(): lax.all_to_all(send_tall, 'face', split_axis=0, concat_axis=1, tiled=True)  16.2 us
    all_to_all x4, waiting for transfers between devices, assemble(): lax.all_to_all(send_flat, 'face', split_axis=0, concat_axis=1, tiled=True)  14.9 us
    all_to_all x4, starting transfers between devices, assemble(): lax.all_to_all(send_flat, 'face', split_axis=0, concat_axis=1, tiled=True)  13.5 us
    all_to_all x4, starting transfers between devices, assemble(): lax.all_to_all(send_tall, 'face', split_axis=0, concat_axis=1, tiled=True)  13.5 us
  transfers between devices with their start and end apart: 30, of which 16 were waited for; matrix products, arithmetic and copies ran while one was open for 5% of the time, Pallas kernels for 0%

commit v1 on v0

--- a/solution.py
+++ b/solution.py
@@ -188,6 +188,10 @@
 
 
 def assemble(values, vector, nbr_face, nbr_edge):
+
+    def feed_the_sections(row_data):
+        return lax.all_gather(row_data, axis_name="fy").sum(axis=0)
+
     summed = in_face(values)
     face_local, row_count, col_count, chan_count = summed.shape
     levels = chan_count // 3
@@ -234,7 +238,7 @@
     flat_lines = flat_lines.reshape(face_local, 2, lax.axis_size("fx"), col_count, chan_count)
     tall_lines = jnp.stack([rim_strips[:, 1], rim_strips[:, 3, ::-1]], axis=1)
     tall_lines = tall_lines.reshape(face_local, 2, lax.axis_size("fy"), row_count, chan_count)
-    flat_whole = lax.psum(flat_lines, "fy")
+    flat_whole = feed_the_sections(flat_lines)
     tall_whole = lax.psum(tall_lines, "fx")
     flat_block = lax.psum_scatter(flat_whole, "fx", scatter_dimension=2, tiled=True)
     tall_block = lax.psum_scatter(tall_whole, "fy", scatter_dimension=2, tiled=True)

time: 373 us -> 374 us (level)
  starting transfers between devices: 69.1 us -> 55 us
  waiting for transfers between devices: 139 us -> 150 us
  other arithmetic: 12.6 us -> 21.6 us
  local copies, waits for them, and re-layouts: 26.4 us -> 21.6 us
    all_gather x0 -> x4, blocking collectives: none -> 33.1 us  [feed_the_sections(): return lax.all_gather(row_data, axis_name='fy').sum(axis=0)]
    psum x3 -> x0, blocking collectives: 31.7 us -> none  [assemble(): flat_whole = lax.psum(flat_lines, 'fy')]
    ppermute x8, waiting for transfers between devices: 0.02 us -> 20.4 us  [padded(): lax.ppermute(head, axis, [((i + 1) % count, i) for i in range(ends)])]
    ppermute x8, starting transfers between devices: 31.5 us -> 17.2 us  [padded(): lax.ppermute(tail, axis, [(i, (i + 1) % count) for i in range(ends)])]
    ppermute x8, waiting for transfers between devices: 5.24 us -> 0.24 us  [padded(): lax.ppermute(tail, axis, [(i, (i + 1) % count) for i in range(ends)])]
    unnamed x33 -> x29, local copies, waits for them, and re-layouts: 10.3 us -> 5.38 us
    unnamed x9, waiting for transfers between devices: 103 us -> 98.3 us
    scatter-add x3, other arithmetic: 0.03 us -> 4.15 us  [assemble(): result = summed.at[:, 0].add(jnp.where(on_south, flat_add, 0.0))]
  transfers between devices with their start and end apart: 30 -> 30, of which waited for: 16 -> 18; matrix products, arithmetic and copies ran while one was open for 5% -> 6% of each run, Pallas kernels for 0% -> 0%
where the time goes in v1:
time: 374 us; the launch traced here: 372 us
  waiting for transfers between devices  150 us (40%)
  blocking collectives  99.8 us (27%)
  starting transfers between devices  55 us (15%)
  local copies, waits for them, and re-layouts  21.6 us (6%)
  other arithmetic  21.6 us (6%)
  between operations  16.4 us (4%)
  matrix products  7.15 us (2%)
    unnamed x9, waiting for transfers between devices  98.3 us
    psum x3, blocking collectives, assemble(): tall_whole = lax.psum(tall_lines, 'fx')  54.8 us
    all_gather x4, blocking collectives, feed_the_sections(): return lax.all_gather(row_data, axis_name='fy').sum(axis=0)  33.1 us
    ppermute x8, waiting for transfers between devices, padded(): lax.ppermute(head, axis, [((i + 1) % count, i) for i in range(ends)])  20.4 us
    ppermute x8, starting transfers between devices, padded(): lax.ppermute(tail, axis, [(i, (i + 1) % count) for i in range(ends)])  17.2 us
    all_to_all x4, waiting for transfers between devices, assemble(): lax.all_to_all(send_flat, 'face', split_axis=0, concat_axis=1, tiled=True)  16.3 us
    all_to_all x4, waiting for transfers between devices, assemble(): lax.all_to_all(send_tall, 'face', split_axis=0, concat_axis=1, tiled=True)  15 us
    all_to_all x4, starting transfers between devices, assemble(): lax.all_to_all(send_flat, 'face', split_axis=0, concat_axis=1, tiled=True)  13.5 us
  transfers between devices with their start and end apart: 30, of which 18 were waited for; matrix products, arithmetic and copies ran while one was open for 6% of the time, Pallas kernels for 0%

profile of v1, /device:TPU:0, one launch (start us, length us, event | category | flops | bytes accessed | tf_op | source)
XLA Modules:
  0.0 372.0 jit_solution(10273628878758850990)
XLA Ops:
  7.4 0.8 fusion.161
  8.1 1.0 slice.770
  13.1 5.0 %collective-permute-start = (f32[3,8,1,192]{3,2,0,1:T(1,128)S(1)}, f32[3,8,1,192]{3,2,0,1:T(1,128)S(1)}, u32[]{:S(2)}, u32[]{:S(2)}) collective-permute-start(f32[3,8,1,192]{3,2,0,1:T(1,128)S(1)} %slice.902), channel_id=1, source_target_pairs={{0,1},{1,2},{2,3},{4,5},{5,6},{6,7},{8,9},{9,10},{10,11},{12,13},{... | collective-permute-start | bytes 55304 | tf_op jit(solution)/shard_map/ppermute | solution.py:19
  18.1 1.3 collective-permute-start.1
  19.5 4.5 %collective-permute-start.4 = (f32[3,8,1,1]{2,1,0,3:T(8,128)S(1)}, f32[3,8,1,1]{2,1,0,3:T(8,128)S(1)}, u32[]{:S(2)}, u32[]{:S(2)}) collective-permute-start(f32[3,8,1,1]{2,1,0,3:T(8,128)S(1)} %get-tuple-element.262), channel_id=1, source_target_pairs={{0,1},{1,2},{2,3},{4,5},{5,6},{6,7},{8,9},{9,10},{10,11},{12,13},{... | collective-permute-start | bytes 296 | tf_op jit(solution)/shard_map/ppermute | solution.py:19
  24.0 1.3 collective-permute-start.5
  30.5 1.3 collective-permute-start.6
  31.8 1.3 collective-permute-start.7
  33.1 3.5 collective-permute-done.7
  37.5 3.2 all-to-all-start.2
  41.4 3.1 all-to-all-done.2
  44.6 3.2 all-to-all-start.3
  48.0 3.7 all-to-all-done.3
  52.9 5.5 %all_gather.13 = f32[4,3,2,4,8,1]{4,3,5,2,1,0:T(4,128)S(1)} all-gather(f32[1,3,2,4,8,1]{4,3,5,2,1,0:T(4,128)S(1)} %bitcast.363), channel_id=1, replica_groups=mesh['face'=2,'fy'=4,'fx'=4] {'fy'}, dimensions={0}, use_global_device_ids=true | all-gather | bytes 3840 | tf_op jit(solution)/shard_map/all_gather | solution.py:193
  58.6 11.9 %all-reduce.4 = f32[3,2,4,8,1]{3,1,4,0,2:T(2,128)S(1)} all-reduce(f32[3,2,4,8,1]{3,1,4,0,2:T(2,128)S(1)} %copy.276), channel_id=5, replica_groups=mesh['face'=2,'fy'=4,'fx'=4] {'fy'}, use_global_device_ids=true, to_apply=%region_7.8.clone | all-reduce | flops 192 | bytes 1536
  70.7 1.3 collective-permute-start.2
  72.0 1.3 collective-permute-start.3
  74.0 1.7 collective-permute-done.3
  76.6 3.4 all-to-all-start.1
  80.1 0.7 broadcast_multiply_fusion.5
  80.8 3.8 %all-to-all-done.1 = f32[6,3,8,192]{3,2,1,0:T(8,128)S(1)} async-done(((f32[6,3,8,192]{3,2,1,0:T(8,128)}), f32[6,3,8,192]{3,2,1,0:T(8,128)S(1)}, u32[]{:S(2)}, u32[]{:S(2)}) %all-to-all-start.1) | async-done | bytes 110624 | tf_op jit(solution)/shard_map/all_to_all | solution.py:219
  84.6 3.4 all-to-all-start
  88.5 4.4 %all-to-all-done = f32[6,3,8,192]{3,2,1,0:T(8,128)S(1)} async-done(((f32[6,3,8,192]{3,2,1,0:T(8,128)}), f32[6,3,8,192]{3,2,1,0:T(8,128)S(1)}, u32[]{:S(2)}, u32[]{:S(2)}) %all-to-all-start) | async-done | bytes 110624 | tf_op jit(solution)/shard_map/all_to_all | solution.py:218
  94.5 9.2 %all_gather.12 = f32[4,3,2,4,8,192]{5,4,3,2,1,0:T(8,128)S(1)} all-gather(f32[1,3,2,4,8,192]{5,4,3,2,1,0:T(8,128)S(1)} %copy.258), channel_id=1, replica_groups=mesh['face'=2,'fy'=4,'fx'=4] {'fy'}, dimensions={0}, use_global_device_ids=true | all-gather | bytes 737280 | tf_op jit(solution)/shard_map/all_gather | solution.py:193
  105.6 34.9 %all-reduce.12.cloned.1.call-done = f32[3,2,4,8,192]{4,3,0,2,1:T(8,128)} async-done(((f32[3,2,4,8,192]{4,3,0,2,1:T(8,128)}), f32[3,2,4,8,192]{4,3,0,2,1:T(8,128)}) %all-reduce.12.cloned.1.call-update) | async-done | bytes 147472
  140.5 1.4 bitcast_dynamic-update-slice_fusion
  141.9 1.4 fusion.100
  143.3 0.8 copy.267
  144.1 18.5 %all-reduce.7 = (f32[3,2,1,8,192]{4,1,3,2,0:T(2,128)S(1)}, f32[3,2,4,8,1]{3,1,4,0,2:T(2,128)S(1)}, f32[3,2,1,8,1]{3,1,4,0,2:T(2,128)S(1)}) all-reduce(f32[3,2,1,8,192]{4,1,3,2,0:T(2,128)S(1)} %copy.267, f32[3,2,4,8,1]{3,1,4,0,2:T(2,128)S(1)} %copy.273, ...), channel_id=1, replica_groups=mesh['face'=2,'fy'=4,'fx'=4] {'fx'}, use_global_device_ids=true, to_apply=%region_2.3 | all-reduce | flops 9456 | bytes 75648 | tf_op jit(solution)/shard_map/psum | solution.py:242
  167.2 1.3 collective-permute-start.8
  168.5 1.5 collective-permute-start.9
  170.0 4.2 %collective-permute-done.9 = f32[3,8,1,192]{3,2,0,1:T(1,128)S(1)} collective-permute-done((f32[3,8,1,192]{3,2,0,1:T(1,128)S(1)}, f32[3,8,1,192]{3,2,0,1:T(1,128)S(1)}, u32[]{:S(2)}, u32[]{:S(2)}) %collective-permute-start.9) | collective-permute-done | bytes 18464 | tf_op jit(solution)/shard_map/ppermute | solution.py:21
  174.3 1.3 collective-permute-start.10
  175.6 1.3 collective-permute-start.11
  176.9 3.4 collective-permute-done.11
  181.3 3.4 all-to-all-start.5
  184.7 0.7 broadcast_multiply_fusion.3
  185.4 3.8 %all-to-all-done.5 = f32[6,3,8,192]{3,2,1,0:T(8,128)S(1)} async-done(((f32[6,3,8,192]{3,2,1,0:T(8,128)}), f32[6,3,8,192]{3,2,1,0:T(8,128)S(1)}, u32[]{:S(2)}, u32[]{:S(2)}) %all-to-all-start.5) | async-done | bytes 110624 | tf_op jit(solution)/shard_map/all_to_all | solution.py:219
  189.2 3.4 all-to-all-start.4
  193.2 4.4 %all-to-all-done.4 = f32[6,3,8,192]{3,2,1,0:T(8,128)S(1)} async-done(((f32[6,3,8,192]{3,2,1,0:T(8,128)}), f32[6,3,8,192]{3,2,1,0:T(8,128)S(1)}, u32[]{:S(2)}, u32[]{:S(2)}) %all-to-all-start.4) | async-done | bytes 110624 | tf_op jit(solution)/shard_map/all_to_all | solution.py:218
  199.2 9.2 %all_gather.14 = f32[4,3,2,4,8,192]{5,4,3,2,1,0:T(8,128)S(1)} all-gather(f32[1,3,2,4,8,192]{5,4,3,2,1,0:T(8,128)S(1)} %copy.300), channel_id=1, replica_groups=mesh['face'=2,'fy'=4,'fx'=4] {'fy'}, dimensions={0}, use_global_device_ids=true | all-gather | bytes 737280 | tf_op jit(solution)/shard_map/all_gather | solution.py:193
  210.2 31.7 %all-reduce.14.cloned.1.call-done = f32[3,2,4,8,192]{4,3,0,2,1:T(8,128)} async-done(((f32[3,2,4,8,192]{4,3,0,2,1:T(8,128)}), f32[3,2,4,8,192]{4,3,0,2,1:T(8,128)}) %all-reduce.14.cloned.1.call-update) | async-done | bytes 147472
  241.9 1.4 fusion.104
  243.3 1.4 fusion.96
  244.7 0.8 copy.308
  245.5 18.2 %psum.34 = f32[3,2,1,8,192]{4,1,3,2,0:T(2,128)S(1)} all-reduce(f32[3,2,1,8,192]{4,1,3,2,0:T(2,128)S(1)} %copy.308), channel_id=1, replica_groups=mesh['face'=2,'fy'=4,'fx'=4] {'fx'}, use_global_device_ids=true, to_apply=%region_10.11 | all-reduce | flops 9216 | bytes 73728 | tf_op jit(solution)/shard_map/psum | solution.py:242
  267.0 1.3 collective-permute-start.12
  268.3 1.3 collective-permute-start.13
  269.8 4.2 %collective-permute-done.13 = f32[3,8,1,192]{3,2,0,1:T(1,128)S(1)} collective-permute-done((f32[3,8,1,192]{3,2,0,1:T(1,128)S(1)}, f32[3,8,1,192]{3,2,0,1:T(1,128)S(1)}, u32[]{:S(2)}, u32[]{:S(2)}) %collective-permute-start.13) | collective-permute-done | bytes 18464 | tf_op jit(solution)/shard_map/ppermute | solution.py:21
  274.1 1.3 collective-permute-start.14
  275.4 1.3 collective-permute-start.15
  276.7 3.4 collective-permute-done.15
  281.0 3.4 all-to-all-start.7
  284.5 0.7 broadcast_multiply_fusion.1
  285.2 3.8 %all-to-all-done.7 = f32[6,3,8,192]{3,2,1,0:T(8,128)S(1)} async-done(((f32[6,3,8,192]{3,2,1,0:T(8,128)}), f32[6,3,8,192]{3,2,1,0:T(8,128)S(1)}, u32[]{:S(2)}, u32[]{:S(2)}) %all-to-all-start.7) | async-done | bytes 110624 | tf_op jit(solution)/shard_map/all_to_all | solution.py:219
  289.0 3.4 all-to-all-start.6
  292.9 4.4 %all-to-all-done.6 = f32[6,3,8,192]{3,2,1,0:T(8,128)S(1)} async-done(((f32[6,3,8,192]{3,2,1,0:T(8,128)}), f32[6,3,8,192]{3,2,1,0:T(8,128)S(1)}, u32[]{:S(2)}, u32[]{:S(2)}) %all-to-all-start.6) | async-done | bytes 110624 | tf_op jit(solution)/shard_map/all_to_all | solution.py:218
  298.9 9.2 %all_gather.15 = f32[4,3,2,4,8,192]{5,4,3,2,1,0:T(8,128)S(1)} all-gather(f32[1,3,2,4,8,192]{5,4,3,2,1,0:T(8,128)S(1)} %copy.320), channel_id=1, replica_groups=mesh['face'=2,'fy'=4,'fx'=4] {'fy'}, dimensions={0}, use_global_device_ids=true | all-gather | bytes 737280 | tf_op jit(solution)/shard_map/all_gather | solution.py:193
  310.0 31.6 %all-reduce.16.cloned.1.call-done = f32[3,2,4,8,192]{4,3,0,2,1:T(8,128)} async-done(((f32[3,2,4,8,192]{4,3,0,2,1:T(8,128)}), f32[3,2,4,8,192]{4,3,0,2,1:T(8,128)}) %all-reduce.16.cloned.1.call-update) | async-done | bytes 147472
  341.6 1.4 fusion.103
  343.0 1.4 fusion.93
  344.4 0.8 copy.326
  345.3 18.2 %psum.35 = f32[3,2,1,8,192]{4,1,3,2,0:T(2,128)S(1)} all-reduce(f32[3,2,1,8,192]{4,1,3,2,0:T(2,128)S(1)} %copy.326), channel_id=1, replica_groups=mesh['face'=2,'fy'=4,'fx'=4] {'fx'}, use_global_device_ids=true, to_apply=%region_14.15 | all-reduce | flops 9216 | bytes 73728 | tf_op jit(solution)/shard_map/psum | solution.py:242
  363.8 0.8 multiply_subtract_fusion
  (256 shorter events, 35.3 us)
Async XLA Ops:
  7.4 19.0 %copy-start = (s32[6,4]{0,1:T(4,128)S(1)}, s32[6,4]{0,1:T(4,128)}, u32[]{:S(2)}) copy-start(s32[6,4]{0,1:T(4,128)} %param.55) | copy-start | bytes 292
  7.4 1.8 copy-start.1
  8.1 1.0 copy-start.3
  9.5 0.7 copy-start.4
  11.2 0.7 copy-start.9
  11.2 0.7 copy-start.2
  12.0 0.7 copy-start.5
  13.1 57.4 %collective-permute-start = (f32[3,8,1,192]{3,2,0,1:T(1,128)S(1)}, f32[3,8,1,192]{3,2,0,1:T(1,128)S(1)}, u32[]{:S(2)}, u32[]{:S(2)}) collective-permute-start(f32[3,8,1,192]{3,2,0,1:T(1,128)S(1)} %slice.902), channel_id=1, source_target_pairs={{0,1},{1,2},{2,3},{4,5},{5,6},{6,7},{8,9},{9,10},{10,11},{12,13},{... | collective-permute-start | bytes 55304 | tf_op jit(solution)/shard_map/ppermute | solution.py:19
  18.1 52.4 %collective-permute-start.1 = (f32[3,8,1,192]{3,2,1,0:T(1,128)S(1)}, f32[3,8,1,192]{3,2,1,0:T(1,128)S(1)}, u32[]{:S(2)}, u32[]{:S(2)}) collective-permute-start(f32[3,8,1,192]{3,2,1,0:T(1,128)S(1)} %slice.903), channel_id=1, source_target_pairs={{1,0},{2,1},{3,2},{5,4},{6,5},{7,6},{9,8},{10,9},{11,10},{13,12},{... | collective-permute-start | bytes 55304 | tf_op jit(solution)/shard_map/ppermute | solution.py:21
  19.5 10.9 %collective-permute-start.4 = (f32[3,8,1,1]{2,1,0,3:T(8,128)S(1)}, f32[3,8,1,1]{2,1,0,3:T(8,128)S(1)}, u32[]{:S(2)}, u32[]{:S(2)}) collective-permute-start(f32[3,8,1,1]{2,1,0,3:T(8,128)S(1)} %get-tuple-element.262), channel_id=1, source_target_pairs={{0,1},{1,2},{2,3},{4,5},{5,6},{6,7},{8,9},{9,10},{10,11},{12,13},{... | collective-permute-start | bytes 296 | tf_op jit(solution)/shard_map/ppermute | solution.py:19
  24.0 6.4 %collective-permute-start.5 = (f32[3,8,1,1]{2,1,0,3:T(8,128)S(1)}, f32[3,8,1,1]{2,1,0,3:T(8,128)S(1)}, u32[]{:S(2)}, u32[]{:S(2)}) collective-permute-start(f32[3,8,1,1]{2,1,0,3:T(8,128)S(1)} %get-tuple-element.263), channel_id=1, source_target_pairs={{1,0},{2,1},{3,2},{5,4},{6,5},{7,6},{9,8},{10,9},{11,10},{13,12},{... | collective-permute-start | bytes 296 | tf_op jit(solution)/shard_map/ppermute | solution.py:21
  25.4 0.7 copy-start.6
  27.6 0.7 copy-start.8
  28.3 0.7 copy-start.7
  30.5 2.6 collective-permute-start.6
  31.8 4.8 %collective-permute-start.7 = (f32[3,1,8,1]{2,1,0,3:T(1,128)S(1)}, f32[3,1,8,1]{2,1,0,3:T(1,128)S(1)}, u32[]{:S(2)}, u32[]{:S(2)}) collective-permute-start(f32[3,1,8,1]{2,1,0,3:T(1,128)S(1)} %get-tuple-element.261), channel_id=1, source_target_pairs={{4,0},{8,4},{12,8},{5,1},{9,5},{13,9},{6,2},{10,6},{14,10},{7,3},{... | collective-permute-start | bytes 296 | tf_op jit(solution)/shard_map/ppermute | solution.py:21
  37.5 7.0 %all-to-all-start.2 = ((f32[6,3,8,1]{2,3,1,0:T(1,128)}), f32[6,3,8,1]{2,3,1,0:T(1,128)S(1)}, u32[]{:S(2)}, u32[]{:S(2)}) async-start(f32[6,3,8,1]{2,3,1,0:T(1,128)} %broadcast_multiply_fusion.7), calls=%async_computation.2 | async-start | bytes 18432 | tf_op jit(solution)/shard_map/all_to_all | solution.py:218
  44.6 7.0 %all-to-all-start.3 = ((f32[6,3,8,1]{2,3,1,0:T(1,128)}), f32[6,3,8,1]{2,3,1,0:T(1,128)S(1)}, u32[]{:S(2)}, u32[]{:S(2)}) async-start(f32[6,3,8,1]{2,3,1,0:T(1,128)} %broadcast_multiply_fusion.6), calls=%async_computation.3 | async-start | bytes 18432 | tf_op jit(solution)/shard_map/all_to_all | solution.py:219
  70.7 3.3 collective-permute-start.2
  72.0 3.7 %collective-permute-start.3 = (f32[3,1,8,192]{3,2,1,0:T(8,128)S(1)}, f32[3,1,8,192]{3,2,1,0:T(8,128)S(1)}, u32[]{:S(2)}, u32[]{:S(2)}) collective-permute-start(f32[3,1,8,192]{3,2,1,0:T(8,128)S(1)} %slice.905), channel_id=1, source_target_pairs={{4,0},{8,4},{12,8},{5,1},{9,5},{13,9},{6,2},{10,6},{14,10},{7,3},{... | collective-permute-start | bytes 55304 | tf_op jit(solution)/shard_map/ppermute | solution.py:21
  76.6 8.0 %all-to-all-start.1 = ((f32[6,3,8,192]{3,2,1,0:T(8,128)}), f32[6,3,8,192]{3,2,1,0:T(8,128)S(1)}, u32[]{:S(2)}, u32[]{:S(2)}) async-start(f32[6,3,8,192]{3,2,1,0:T(8,128)} %broadcast_multiply_fusion.4), calls=%async_computation.1 | async-start | bytes 294912 | tf_op jit(solution)/shard_map/all_to_all | solution.py:219
  84.6 8.3 %all-to-all-start = ((f32[6,3,8,192]{3,2,1,0:T(8,128)}), f32[6,3,8,192]{3,2,1,0:T(8,128)S(1)}, u32[]{:S(2)}, u32[]{:S(2)}) async-start(f32[6,3,8,192]{3,2,1,0:T(8,128)} %broadcast_multiply_fusion.5), calls=%async_computation | async-start | bytes 294912 | tf_op jit(solution)/shard_map/all_to_all | solution.py:218
  88.0 52.4 %all-reduce.12.cloned.1.call-start = ((), (), s32[]{:S(2)}) async-start(), calls=%async_computation.14 | async-start | bytes 393216
  104.5 38.7 %reduce-scatter.7.cloned.1.call-start = ((), (), s32[]{:S(2)}) async-start(), calls=%async_computation.11 | async-start | bytes 245760 | tf_op jit(solution)/shard_map/reduce_scatter | solution.py:244
  167.2 2.8 collective-permute-start.8
  168.5 5.7 %collective-permute-start.9 = (f32[3,8,1,192]{3,2,0,1:T(1,128)S(1)}, f32[3,8,1,192]{3,2,0,1:T(1,128)S(1)}, u32[]{:S(2)}, u32[]{:S(2)}) collective-permute-start(f32[3,8,1,192]{3,2,0,1:T(1,128)S(1)} %get-tuple-element.231), channel_id=1, source_target_pairs={{1,0},{2,1},{3,2},{5,4},{6,5},{7,6},{9,8},{10,9},{11,10},{13,12},{... | collective-permute-start | bytes 55304 | tf_op jit(solution)/shard_map/ppermute | solution.py:21
  174.3 2.6 collective-permute-start.10
  175.6 4.7 %collective-permute-start.11 = (f32[3,1,8,192]{3,2,0,1:T(8,128)S(1)}, f32[3,1,8,192]{3,2,0,1:T(8,128)S(1)}, u32[]{:S(2)}, u32[]{:S(2)}) collective-permute-start(f32[3,1,8,192]{3,2,0,1:T(8,128)S(1)} %get-tuple-element.229), channel_id=1, source_target_pairs={{4,0},{8,4},{12,8},{5,1},{9,5},{13,9},{6,2},{10,6},{14,10},{7,3},{... | collective-permute-start | bytes 55304 | tf_op jit(solution)/shard_map/ppermute | solution.py:21
  181.3 8.0 %all-to-all-start.5 = ((f32[6,3,8,192]{3,2,1,0:T(8,128)}), f32[6,3,8,192]{3,2,1,0:T(8,128)S(1)}, u32[]{:S(2)}, u32[]{:S(2)}) async-start(f32[6,3,8,192]{3,2,1,0:T(8,128)} %broadcast_multiply_fusion.2), calls=%async_computation.5 | async-start | bytes 294912 | tf_op jit(solution)/shard_map/all_to_all | solution.py:219
  189.2 8.3 %all-to-all-start.4 = ((f32[6,3,8,192]{3,2,1,0:T(8,128)}), f32[6,3,8,192]{3,2,1,0:T(8,128)S(1)}, u32[]{:S(2)}, u32[]{:S(2)}) async-start(f32[6,3,8,192]{3,2,1,0:T(8,128)} %broadcast_multiply_fusion.3), calls=%async_computation.4 | async-start | bytes 294912 | tf_op jit(solution)/shard_map/all_to_all | solution.py:218
  192.7 49.2 %all-reduce.14.cloned.1.call-start = ((), (), s32[]{:S(2)}) async-start(), calls=%async_computation.15 | async-start | bytes 393216
  209.2 35.5 %reduce-scatter.9.cloned.1.call-start = ((), (), s32[]{:S(2)}) async-start(), calls=%async_computation.12 | async-start | bytes 245760 | tf_op jit(solution)/shard_map/reduce_scatter | solution.py:244
  267.0 2.8 collective-permute-start.12
  268.3 5.7 %collective-permute-start.13 = (f32[3,8,1,192]{3,2,0,1:T(1,128)S(1)}, f32[3,8,1,192]{3,2,0,1:T(1,128)S(1)}, u32[]{:S(2)}, u32[]{:S(2)}) collective-permute-start(f32[3,8,1,192]{3,2,0,1:T(1,128)S(1)} %get-tuple-element.227), channel_id=1, source_target_pairs={{1,0},{2,1},{3,2},{5,4},{6,5},{7,6},{9,8},{10,9},{11,10},{13,12},{... | collective-permute-start | bytes 55304 | tf_op jit(solution)/shard_map/ppermute | solution.py:21
  274.1 2.6 collective-permute-start.14
  275.4 4.7 %collective-permute-start.15 = (f32[3,1,8,192]{3,2,0,1:T(8,128)S(1)}, f32[3,1,8,192]{3,2,0,1:T(8,128)S(1)}, u32[]{:S(2)}, u32[]{:S(2)}) collective-permute-start(f32[3,1,8,192]{3,2,0,1:T(8,128)S(1)} %get-tuple-element.225), channel_id=1, source_target_pairs={{4,0},{8,4},{12,8},{5,1},{9,5},{13,9},{6,2},{10,6},{14,10},{7,3},{... | collective-permute-start | bytes 55304 | tf_op jit(solution)/shard_map/ppermute | solution.py:21
  281.0 8.0 %all-to-all-start.7 = ((f32[6,3,8,192]{3,2,1,0:T(8,128)}), f32[6,3,8,192]{3,2,1,0:T(8,128)S(1)}, u32[]{:S(2)}, u32[]{:S(2)}) async-start(f32[6,3,8,192]{3,2,1,0:T(8,128)} %broadcast_multiply_fusion), calls=%async_computation.7 | async-start | bytes 294912 | tf_op jit(solution)/shard_map/all_to_all | solution.py:219
  289.0 8.3 %all-to-all-start.6 = ((f32[6,3,8,192]{3,2,1,0:T(8,128)}), f32[6,3,8,192]{3,2,1,0:T(8,128)S(1)}, u32[]{:S(2)}, u32[]{:S(2)}) async-start(f32[6,3,8,192]{3,2,1,0:T(8,128)} %broadcast_multiply_fusion.1), calls=%async_computation.6 | async-start | bytes 294912 | tf_op jit(solution)/shard_map/all_to_all | solution.py:218
  292.4 49.2 %all-reduce.16.cloned.1.call-start = ((), (), s32[]{:S(2)}) async-start(), calls=%async_computation.16 | async-start | bytes 393216
  308.9 35.5 %reduce-scatter.11.cloned.1.call-start = ((), (), s32[]{:S(2)}) async-start(), calls=%async_computation.13 | async-start | bytes 245760 | tf_op jit(solution)/shard_map/reduce_scatter | solution.py:244
Sparse Core Ops, SparseCore 0:
  104.7 35.7 all-reduce.11
  209.3 32.5 all-reduce.13
  309.1 32.5 all-reduce.15
Sparse Core Ops, SparseCore 1:
  107.5 20.6 reduce-scatter.6
  212.1 17.3 reduce-scatter.8
  311.9 17.3 reduce-scatter.10
